TPU v7x, 32 devices: a whole 2x2x4 slice. The times are simulated.
32 devices in a mesh: expert: 8 (over y, x, core), replica: 4 (over z).
Axes of the slice: x: 2, y: 2, z: 4, core: 2. Of those that a mesh axis runs over, the one named last changes fastest.
Arguments:
- tokens_in: bfloat16 [8192, 2048], P(('expert', 'replica')), may hold values from -6 to 6
- cotangents: bfloat16 [8192, 8192], P(('expert', 'replica')), may hold values from -0.1796875 to 0.1796875
- left_root: bfloat16 [8, 2048, 2048], P('expert'), may hold values from -2 to 6, as said below
- right_root: bfloat16 [8, 8, 1024, 1024], P('expert', 'replica'), may hold values from -2 to 6, as said below
Outputs:
- update: bfloat16 [8, 2048, 8192], P('expert', None, 'replica')
Inputs may be any that keep to these rules, and one draw needn't show every extreme that they name: `left_root`: each matrix is symmetric. `right_root`: each block is symmetric.
All inputs are finite; a program needn't handle non-finite values.
Results may differ from a plain program's by a relative error of at most 0.0058.
Values may be sent and summed in bfloat16 or wider, within the bound.
A program may use at most 192 MiB of HBM per device.

v0:
```python
import jax
import jax.numpy as jnp
from jax import lax
from jax.sharding import PartitionSpec as P


def body(tokens_in, cotangents, left_root, right_root):
    expert_count = lax.axis_size("expert")
    replica_count = lax.axis_size("replica")
    local_experts = left_root.shape[0]
    width = left_root.shape[1]
    block_count = right_root.shape[1]
    block_size = right_root.shape[2]
    columns = cotangents.shape[1] // replica_count
    slot_count = tokens_in.shape[0] // (expert_count * local_experts)
    shaped = cotangents.reshape(1, expert_count, local_experts, slot_count, replica_count, columns)
    routed = lax.all_to_all(
        lax.all_to_all(shaped, "expert", split_axis=1, concat_axis=1, tiled=True),
        "replica",
        split_axis=4,
        concat_axis=0,
        tiled=True,
    )
    routed = routed.reshape(replica_count, expert_count, local_experts, slot_count, columns)
    tokens = tokens_in.reshape(expert_count, local_experts, slot_count, width)
    grouped = lax.all_to_all(tokens, "expert", split_axis=0, concat_axis=0, tiled=True)
    gradient = jnp.einsum(
        "rnxsd,rnxsf->xdf",
        lax.all_gather(grouped[None], "replica", axis=0, tiled=True),
        routed,
        preferred_element_type=jnp.float32,
    )
    gradient = gradient.astype(jnp.bfloat16)
    blocks = gradient.reshape(local_experts, width, block_count, block_size)
    applied = jnp.einsum("xdbk,xbkj->xdbj", blocks, right_root, preferred_element_type=jnp.float32)
    applied = applied.astype(jnp.bfloat16).reshape(local_experts, width, columns)
    update = jnp.einsum("xde,xef->xdf", left_root, applied, preferred_element_type=jnp.float32)
    return update.astype(jnp.bfloat16)


def solution(mesh):
    in_specs = (
        P(("expert", "replica"), None),
        P(("expert", "replica"), None),
        P("expert", None, None),
        P("expert", "replica", None, None),
    )
    out_specs = P("expert", None, "replica")
    return jax.shard_map(body, mesh=mesh, in_specs=in_specs, out_specs=out_specs, check_vma=False)
```

profile of v0, /device:TPU:0, one launch (start us, length us, event | category | flops | bytes accessed | tf_op | source)
XLA Modules:
  0.0 275.7 jit_solution(12691857189009747764)
XLA Ops:
  6.5 5.2 %all-to-all-start = ((bf16[8,1,32,2048]{3,2,1,0:T(8,128)(2,1)}), bf16[8,1,32,2048]{3,2,1,0:T(8,128)(2,1)S(1)}, u32[]{:S(2)}, u32[]{:S(2)}) async-start(bf16[8,1,32,2048]{3,2,1,0:T(8,128)(2,1)} %bitcast.41), calls=%async_computation | async-start | bytes 2097152 | tf_op jit(solution)/shard_map/all_to_all | solution.py:26
  11.7 7.8 %reshape.40 = bf16[1,8,1,32,4,2048]{5,4,3,1,2,0:T(4,128)(2,1)} reshape(bf16[256,8192]{1,0:T(8,128)(2,1)} %param.5) | data formatting | bytes 8388608 | tf_op jit(solution)/shard_map/reshape | solution.py:16
  19.5 6.6 %copy.13 = bf16[1,8,1,32,4,2048]{5,3,4,2,0,1:T(8,128)(2,1)} copy(bf16[1,8,1,32,4,2048]{5,4,3,1,2,0:T(4,128)(2,1)} %reshape.40) | data formatting | bytes 8388608 | tf_op jit(solution)/shard_map/reshape | solution.py:16
  26.1 1.0 all-to-all-done
  27.1 0.0 copy-start
  27.1 4.6 %all-to-all-start.1 = ((bf16[1,8,1,32,4,2048]{5,3,4,2,0,1:T(8,128)(2,1)}), bf16[1,8,1,32,4,2048]{5,3,4,2,0,1:T(8,128)(2,1)}, u32[]{:S(2)}, u32[]{:S(2)}) async-start(bf16[1,8,1,32,4,2048]{5,3,4,2,0,1:T(8,128)(2,1)} %copy.13), calls=%async_computation.1 | async-start | bytes 8388608 | tf_op jit(solution)/shard_map/all_to_all | solution.py:18
  31.7 0.0 all-gather.3.cloned.1.call-start
  31.8 0.0 copy-done
  31.8 0.7 all-gather.3.cloned.1.call-update
  32.4 48.4 %all-to-all-done.1 = bf16[1,8,1,32,4,2048]{5,3,4,2,0,1:T(8,128)(2,1)} async-done(((bf16[1,8,1,32,4,2048]{5,3,4,2,0,1:T(8,128)(2,1)}), bf16[1,8,1,32,4,2048]{5,3,4,2,0,1:T(8,128)(2,1)}, u32[]{:S(2)}, u32[]{:S(2)}) %all-to-all-start.1) | async-done | bytes 4194336 | tf_op jit(solution)/shard_map/all_to_all | solution.py:18
  80.8 4.8 %copy.14 = bf16[1,8,1,32,4,2048]{5,3,1,2,0,4:T(8,128)(2,1)} copy(bf16[1,8,1,32,4,2048]{5,3,4,2,0,1:T(8,128)(2,1)} %all-to-all-done.1) | data formatting | bytes 8388608 | tf_op jit(solution)/shard_map/all_to_all | solution.py:18
  85.6 5.0 %all-to-all-start.2 = ((bf16[1,8,1,32,4,2048]{5,3,1,2,0,4:T(8,128)(2,1)}), bf16[1,8,1,32,4,2048]{5,3,1,2,0,4:T(8,128)(2,1)}, u32[]{:S(2)}, u32[]{:S(2)}) async-start(bf16[1,8,1,32,4,2048]{5,3,1,2,0,4:T(8,128)(2,1)} %copy.14), calls=%async_computation.2 | async-start | bytes 8388608 | tf_op jit(solution)/shard_map/all_to_all | solution.py:17
  90.6 61.0 %all-gather.3.cloned.1.call-done = bf16[32,1,32,2048]{3,2,1,0:T(8,128)(2,1)} async-done(((bf16[8,1,32,2048]{3,2,1,0:T(8,128)(2,1)}), bf16[32,1,32,2048]{3,2,1,0:T(8,128)(2,1)}) %all-gather.3.cloned.1.call-update) | async-done | bytes 4194320 | tf_op jit(solution)/shard_map/all_gather | solution.py:29
  151.6 54.4 %all-to-all-done.2 = bf16[1,8,1,32,4,2048]{5,3,1,2,0,4:T(8,128)(2,1)} async-done(((bf16[1,8,1,32,4,2048]{5,3,1,2,0,4:T(8,128)(2,1)}), bf16[1,8,1,32,4,2048]{5,3,1,2,0,4:T(8,128)(2,1)}, u32[]{:S(2)}, u32[]{:S(2)}) %all-to-all-start.2) | async-done | bytes 4194336 | tf_op jit(solution)/shard_map/all_to_all | solution.py:17
  205.9 0.0 slice-start
  205.9 14.1 %bitcast_convert_fusion = bf16[2048,2048]{0,1:T(8,128)(2,1)} fusion(bf16[1,8,1,32,4,2048]{5,3,1,2,0,4:T(8,128)(2,1)} %all-to-all-done.2, bf16[4,8,32,2048]{3,2,1,0:T(8,128)(2,1)} %bitcast.44), kind=kOutput, calls=%fused_computation | convolution fusion | flops 8594128896 | bytes 16777216 | tf_op jit(solution)/shard_map/rnxsd,rnxsf->xdf/dot_general | solution.py:27
  220.1 0.0 slice-start.1
  220.1 14.8 %convolution_convert_fusion = bf16[2,2048,1024]{1,2,0:T(8,128)(2,1)} fusion(bf16[2048,2,1024]{0,2,1:T(8,128)(2,1)} %bitcast.45, bf16[1,2,1024,1024]{3,2,1,0:T(8,128)(2,1)} %param.7), kind=kOutput, calls=%fused_computation.4 | convolution fusion | flops 8594128896 | bytes 20971520 | tf_op jit(solution)/shard_map/xdbk,xbkj->xdbj/dot_general | solution.py:35
  234.9 0.0 slice-done
  234.9 0.0 slice-done.1
  234.9 21.8 %convert_bitcast_fusion = bf16[1,2048,2048]{1,2,0:T(8,128)(2,1)} fusion(bf16[2048,2048]{0,1:T(8,128)(2,1)} %bitcast.46, bf16[1,2048,2048]{2,1,0:T(8,128)(2,1)S(1)} %bitcast.43), kind=kOutput, calls=%fused_computation.3 | convolution fusion | flops 17184063488 | bytes 25165824 | tf_op jit(solution)/shard_map/xde,xef->xdf/dot_general | solution.py:37
  256.7 12.2 %copy.19 = bf16[1,2048,2048]{2,1,0:T(8,128)(2,1)} copy(bf16[1,2048,2048]{1,2,0:T(8,128)(2,1)} %convert_bitcast_fusion) | data formatting | bytes 16777216 | tf_op jit(solution)/shard_map/convert_element_type | solution.py:38
  (1 shorter events, 0.0 us)
Async XLA Ops:
  6.5 20.6 %all-to-all-start = ((bf16[8,1,32,2048]{3,2,1,0:T(8,128)(2,1)}), bf16[8,1,32,2048]{3,2,1,0:T(8,128)(2,1)S(1)}, u32[]{:S(2)}, u32[]{:S(2)}) async-start(bf16[8,1,32,2048]{3,2,1,0:T(8,128)(2,1)} %bitcast.41), calls=%async_computation | async-start | bytes 2097152 | tf_op jit(solution)/shard_map/all_to_all | solution.py:26
  27.1 4.6 %copy-start = (bf16[8,1,32,2048]{3,2,1,0:T(8,128)(2,1)}, bf16[8,1,32,2048]{3,2,1,0:T(8,128)(2,1)S(1)}, u32[]{:S(2)}) copy-start(bf16[8,1,32,2048]{3,2,1,0:T(8,128)(2,1)S(1)} %all-to-all-done) | copy-start | bytes 3145732
  27.1 53.7 %all-to-all-start.1 = ((bf16[1,8,1,32,4,2048]{5,3,4,2,0,1:T(8,128)(2,1)}), bf16[1,8,1,32,4,2048]{5,3,4,2,0,1:T(8,128)(2,1)}, u32[]{:S(2)}, u32[]{:S(2)}) async-start(bf16[1,8,1,32,4,2048]{5,3,4,2,0,1:T(8,128)(2,1)} %copy.13), calls=%async_computation.1 | async-start | bytes 8388608 | tf_op jit(solution)/shard_map/all_to_all | solution.py:18
  31.7 119.9 %all-gather.3.cloned.1.call-start = ((), (), s32[]{:S(2)}) async-start(), calls=%async_computation.3 | async-start | bytes 5242880 | tf_op jit(solution)/shard_map/all_gather | solution.py:29
  85.6 120.3 %all-to-all-start.2 = ((bf16[1,8,1,32,4,2048]{5,3,1,2,0,4:T(8,128)(2,1)}), bf16[1,8,1,32,4,2048]{5,3,1,2,0,4:T(8,128)(2,1)}, u32[]{:S(2)}, u32[]{:S(2)}) async-start(bf16[1,8,1,32,4,2048]{5,3,1,2,0,4:T(8,128)(2,1)} %copy.14), calls=%async_computation.2 | async-start | bytes 8388608 | tf_op jit(solution)/shard_map/all_to_all | solution.py:17
  205.9 28.9 %slice-start = ((s8[8388608]{0:T(1024)(128)(4,1)}), s8[4194304]{0:T(1024)(128)(4,1)S(1)}, s32[]{:S(2)}) async-start(s8[8388608]{0:T(1024)(128)(4,1)} %bitcast.42), calls=%async_computation.4 | async-start | bytes 8388608
  220.1 14.8 %slice-start.1 = ((s8[8388608]{0:T(1024)(128)(4,1)}), s8[4194304]{0:T(1024)(128)(4,1)S(1)}, s32[]{:S(2)}) async-start(s8[8388608]{0:T(1024)(128)(4,1)} %bitcast.42), calls=%async_computation.5 | async-start | bytes 8388608
Sparse Core Ops, SparseCore 0:
  34.1 117.4 all-gather.2
where the time goes:
time: 277 us; the launch traced here: 276 us
  waiting for transfers between devices  165 us (60%)
  matrix products  50.7 us (18%)
  local copies, waits for them, and re-layouts  31.4 us (11%)
  starting transfers between devices  14.8 us (5%)
  between operations  13.4 us (5%)
    all_gather x1, waiting for transfers between devices, body(): lax.all_gather(grouped[None], 'replica', axis=0, tiled=True)  61 us
    all_to_all x1, waiting for transfers between devices, body(): lax.all_to_all(lax.all_to_all(shaped, 'expert', split_axis=1, concat_axis...  54.4 us
    all_to_all x1, waiting for transfers between devices, body(): lax.all_to_all(shaped, 'expert', split_axis=1, concat_axis=1, tiled=True)  48.4 us
    dot_general x1, matrix products, body(): jnp.einsum('xde,xef->xdf', left_root, applied, preferred_element_type=jnp...  21.8 us
    dot_general x1, matrix products, body(): jnp.einsum('xdbk,xbkj->xdbj', blocks, right_root, preferred_element_type=...  14.8 us
    reshape x2, local copies, waits for them, and re-layouts, body(): cotangents.reshape(1, expert_count, local_experts, slot_count, replica_co...  14.4 us
    dot_general x1, matrix products, body(): jnp.einsum('rnxsd,rnxsf->xdf', lax.all_gather(grouped[None], 'replica', a...  14.1 us
    convert_element_type x1, local copies, waits for them, and re-layouts, body(): return update.astype(jnp.bfloat16)  12.2 us
  transfers between devices with their start and end apart: 4, of which 4 were waited for; matrix products, arithmetic and copies ran while one was open for 7% of the time, Pallas kernels for 0%

commit v1 on v0

--- a/solution.py
+++ b/solution.py
@@ -24,12 +24,41 @@
     routed = routed.reshape(replica_count, expert_count, local_experts, slot_count, columns)
     tokens = tokens_in.reshape(expert_count, local_experts, slot_count, width)
     grouped = lax.all_to_all(tokens, "expert", split_axis=0, concat_axis=0, tiled=True)
+    size, index, width_2 = (
+        lax.axis_size("replica"),
+        lax.axis_index("replica"),
+        grouped[None].shape[0],
+    )
+    right = [(i, (i + 1) % size) for i in range(size)]
+    behind = [(i, (i - 1) % size) for i in range(size)]
+    halfway = size // 2
+    from_left = from_right = grouped[None]
     gradient = jnp.einsum(
         "rnxsd,rnxsf->xdf",
-        lax.all_gather(grouped[None], "replica", axis=0, tiled=True),
-        routed,
+        grouped[None],
+        lax.dynamic_slice_in_dim(routed, index * width_2, grouped[None].shape[0], axis=0),
         preferred_element_type=jnp.float32,
     )
+    for step in range(1, halfway + 1):
+        from_left = lax.ppermute(from_left, "replica", right)
+        if step < size - halfway:
+            from_right = lax.ppermute(from_right, "replica", behind)
+            gradient = gradient + jnp.einsum(
+                "rnxsd,rnxsf->xdf",
+                from_right,
+                lax.dynamic_slice_in_dim(
+                    routed, (index + step) % size * width_2, from_right.shape[0], axis=0
+                ),
+                preferred_element_type=jnp.float32,
+            )
+        gradient = gradient + jnp.einsum(
+            "rnxsd,rnxsf->xdf",
+            from_left,
+            lax.dynamic_slice_in_dim(
+                routed, (index - step) % size * width_2, from_left.shape[0], axis=0
+            ),
+            preferred_element_type=jnp.float32,
+        )
     gradient = gradient.astype(jnp.bfloat16)
     blocks = gradient.reshape(local_experts, width, block_count, block_size)
     applied = jnp.einsum("xdbk,xbkj->xdbj", blocks, right_root, preferred_element_type=jnp.float32)

time: 277 us -> 328 us (1.18)
  waiting for transfers between devices: 165 us -> 102 us
  blocking collectives: 0 us -> 54.1 us
  starting transfers between devices: 14.8 us -> 52.2 us
  matrix products: 50.7 us -> 85.7 us
  between operations: 13.4 us -> 0.03 us
    ppermute x0 -> x3, waiting for transfers between devices: none -> 91.6 us  [the longest x2 91.6 us: body(): from_left = lax.ppermute(from_left, 'replica', right)]
    all_gather x1 -> x0, waiting for transfers between devices: 61 us -> none  [body(): lax.all_gather(grouped[None], 'replica', axis=0, tiled=True)]
    all_to_all x1, waiting for transfers between devices: 54.4 us -> 0.01 us  [body(): lax.all_to_all(lax.all_to_all(shaped, 'expert', split_axis=1, concat_axis...]
    all_to_all x0 -> x1, blocking collectives: none -> 54.1 us  [body(): lax.all_to_all(shaped, 'expert', split_axis=1, concat_axis=1, tiled=True)]
    all_to_all x1 -> x0, waiting for transfers between devices: 48.4 us -> none  [body(): lax.all_to_all(shaped, 'expert', split_axis=1, concat_axis=1, tiled=True)]
    ppermute x0 -> x3, starting transfers between devices: none -> 43.8 us  [the longest x2 42 us: body(): from_left = lax.ppermute(from_left, 'replica', right)]
    dot_general x1 -> x4, matrix products: 14.1 us -> 49.5 us  [the longest x2 30.4 us: body(): jnp.einsum('rnxsd,rnxsf->xdf', from_left, lax.dynamic_slice_in_dim(routed...]
    all_to_all x1, waiting for transfers between devices: 1 us -> 10.5 us  [body(): lax.all_to_all(tokens, 'expert', split_axis=0, concat_axis=0, tiled=True)]
  transfers between devices with their start and end apart: 4 -> 5, of which waited for: 4 -> 2; matrix products, arithmetic and copies ran while one was open for 7% -> 10% of each run, Pallas kernels for 0% -> 0%
where the time goes in v1:
time: 328 us; the launch traced here: 324 us
  waiting for transfers between devices  102 us (31%)
  matrix products  85.7 us (26%)
  blocking collectives  54.1 us (16%)
  starting transfers between devices  52.2 us (16%)
  local copies, waits for them, and re-layouts  29.4 us (9%)
    ppermute x2, waiting for transfers between devices, body(): from_left = lax.ppermute(from_left, 'replica', right)  91.6 us
    all_to_all x1, blocking collectives, body(): lax.all_to_all(shaped, 'expert', split_axis=1, concat_axis=1, tiled=True)  54.1 us
    ppermute x2, starting transfers between devices, body(): from_left = lax.ppermute(from_left, 'replica', right)  42 us
    dot_general x2, matrix products, body(): jnp.einsum('rnxsd,rnxsf->xdf', from_left, lax.dynamic_slice_in_dim(routed...  30.4 us
    dot_general x1, matrix products, body(): jnp.einsum('xde,xef->xdf', left_root, applied, preferred_element_type=jnp...  21.5 us
    dot_general x1, matrix products, body(): jnp.einsum('xdbk,xbkj->xdbj', blocks, right_root, preferred_element_type=...  14.6 us
    reshape x2, local copies, waits for them, and re-layouts, body(): cotangents.reshape(1, expert_count, local_experts, slot_count, replica_co...  12.4 us
    convert_element_type x1, local copies, waits for them, and re-layouts, body(): return update.astype(jnp.bfloat16)  12.2 us
  transfers between devices with their start and end apart: 5, of which 2 were waited for; matrix products, arithmetic and copies ran while one was open for 10% of the time, Pallas kernels for 0%

profile of v1, /device:TPU:0, one launch (start us, length us, event | category | flops | bytes accessed | tf_op | source)
XLA Modules:
  0.0 323.7 jit_solution(10526201283825209460)
XLA Ops:
  0.0 7.8 %reshape.86 = bf16[1,8,1,32,4,2048]{5,4,3,1,2,0:T(4,128)(2,1)} reshape(bf16[256,8192]{1,0:T(8,128)(2,1)} %param.5) | data formatting | bytes 8388608 | tf_op jit(solution)/shard_map/reshape | solution.py:16
  7.8 4.6 %copy.13 = bf16[1,8,1,32,4,2048]{5,3,4,2,0,1:T(8,128)(2,1)S(1)} copy(bf16[1,8,1,32,4,2048]{5,4,3,1,2,0:T(4,128)(2,1)} %reshape.86) | data formatting | bytes 8388608 | tf_op jit(solution)/shard_map/reshape | solution.py:16
  12.4 54.1 %all_to_all.19 = bf16[1,8,1,32,4,2048]{5,3,4,2,0,1:T(8,128)(2,1)} all-to-all(bf16[1,8,1,32,4,2048]{5,3,4,2,0,1:T(8,128)(2,1)S(1)} %copy.13), channel_id=1, replica_groups=mesh['expert'=8,'replica'=4] {'expert'}, dimensions={1} | all-to-all | bytes 8388608 | tf_op jit(solution)/shard_map/all_to_all | solution.py:18
  66.5 3.6 %all-to-all-start.2 = ((bf16[8,1,32,2048]{3,2,1,0:T(8,128)(2,1)}), bf16[8,1,32,2048]{3,2,1,0:T(8,128)(2,1)S(1)}, u32[]{:S(2)}, u32[]{:S(2)}) async-start(bf16[8,1,32,2048]{3,2,1,0:T(8,128)(2,1)} %bitcast.1), calls=%async_computation.2 | async-start | bytes 2097152 | tf_op jit(solution)/shard_map/all_to_all | solution.py:26
  70.1 4.8 %copy.14 = bf16[1,8,1,32,4,2048]{5,3,1,2,0,4:T(8,128)(2,1)} copy(bf16[1,8,1,32,4,2048]{5,3,4,2,0,1:T(8,128)(2,1)} %all_to_all.19) | data formatting | bytes 8388608 | tf_op jit(solution)/shard_map/all_to_all | solution.py:18
  74.9 10.5 %all-to-all-done.2 = bf16[8,1,32,2048]{3,2,1,0:T(8,128)(2,1)S(1)} async-done(((bf16[8,1,32,2048]{3,2,1,0:T(8,128)(2,1)}), bf16[8,1,32,2048]{3,2,1,0:T(8,128)(2,1)S(1)}, u32[]{:S(2)}, u32[]{:S(2)}) %all-to-all-start.2) | async-done | bytes 1048608 | tf_op jit(solution)/shard_map/all_to_all | solution.py:26
  85.4 4.9 %all-to-all-start.1 = ((bf16[1,8,1,32,4,2048]{5,3,1,2,0,4:T(8,128)(2,1)}), bf16[1,8,1,32,4,2048]{5,3,1,2,0,4:T(8,128)(2,1)}, u32[]{:S(2)}, u32[]{:S(2)}) async-start(bf16[1,8,1,32,4,2048]{5,3,1,2,0,4:T(8,128)(2,1)} %copy.14), calls=%async_computation.1 | async-start | bytes 8388608 | tf_op jit(solution)/shard_map/all_to_all | solution.py:17
  90.3 2.0 collective-permute-start.1
  92.3 1.9 collective-permute-start
  94.2 91.6 %collective-permute-done.1 = bf16[1,8,1,32,2048]{4,3,1,2,0:T(8,128)(2,1)S(1)} collective-permute-done((bf16[1,8,1,32,2048]{4,3,1,2,0:T(8,128)(2,1)S(1)}, bf16[1,8,1,32,2048]{4,3,1,2,0:T(8,128)(2,1)S(1)}, u32[]{:S(2)}, u32[]{:S(2)}) %collective-permute-start.1) | collective-permute-done | bytes 1048608 | tf_op jit(solution)/shard_map/ppermute | solution.py:43
  185.8 39.9 %collective-permute-start.2 = (bf16[1,8,1,32,2048]{4,3,1,2,0:T(8,128)(2,1)S(1)}, bf16[1,8,1,32,2048]{4,3,1,2,0:T(8,128)(2,1)}, u32[]{:S(2)}, u32[]{:S(2)}) collective-permute-start(bf16[1,8,1,32,2048]{4,3,1,2,0:T(8,128)(2,1)S(1)} %collective-permute-done.1), channel_id=1, source_target_pairs={{0,1},{1,2},{2,3},{3,0},{4,5},{5,6},{6,7},{7,4},{8,9},{9,10},{10,1... | collective-permute-start | bytes 3145736 | tf_op jit(solution)/shard_map/ppermute | solution.py:43
  225.7 0.0 all-to-all-done.1
  225.7 9.4 %fusion.8 = f32[2048,2048,1]{1,0,2:T(8,128)} fusion(bf16[1,8,1,32,2048]{4,3,1,2,0:T(8,128)(2,1)S(1)} %collective-permute-done.1, bf16[1,8,1,32,4,2048]{5,3,1,2,0,4:T(8,128)(2,1)} %all-to-all-done.1, s32[]{:T(128)S(6)} %select_n.31), kind=kOutput, calls=%fused_computation.11 | convolution fusion | flops 2147483648 | bytes 18874372 | tf_op jit(solution)/shard_map/rnxsd,rnxsf->xdf/dot_general | solution.py:54
  235.1 9.3 %fusion.14 = f32[2048,2048,1]{1,0,2:T(8,128)} fusion(bf16[8,1,32,2048]{3,2,1,0:T(8,128)(2,1)S(1)} %all-to-all-done.2, bf16[1,8,1,32,4,2048]{5,3,1,2,0,4:T(8,128)(2,1)} %all-to-all-done.1, s32[]{:T(128)S(6)} %select_n.27), kind=kOutput, calls=%fused_computation.17 | convolution fusion | flops 2147483648 | bytes 18874372 | tf_op jit(solution)/shard_map/rnxsd,rnxsf->xdf/dot_general | solution.py:36
  244.4 0.0 collective-permute-done
  244.4 0.0 slice-start
  244.4 9.8 %fusion.11 = f32[2048,2048,1]{1,0,2:T(8,128)} fusion(bf16[1,8,1,32,2048]{4,3,1,2,0:T(8,128)(2,1)} %collective-permute-done, bf16[1,8,1,32,4,2048]{5,3,1,2,0,4:T(8,128)(2,1)} %all-to-all-done.1, s32[]{:T(128)S(6)} %select_n.29), kind=kOutput, calls=%fused_computation.14 | convolution fusion | flops 2147483648 | bytes 18874372 | tf_op jit(solution)/shard_map/rnxsd,rnxsf->xdf/dot_general | solution.py:46
  254.2 0.0 slice-start.1
  254.2 0.0 collective-permute-done.2
  254.2 21.1 %fusion = bf16[2048,2048]{1,0:T(8,128)(2,1)} fusion(f32[2048,2048,1]{1,0,2:T(8,128)} %fusion.8, f32[2048,2048,1]{1,0,2:T(8,128)} %fusion.11, f32[2048,2048,1]{1,0,2:T(8,128)} %fusion.14, bf16[1,8,1,32,2048]{4,3,1,2,0:T(8,128)(2,1)} %collective-permute-done.2, bf16[1,8,1,32,4,2048]{5,3,1,2,0,4:T(8,128)(2,1)} %all-to-all-done.1, s32[]{:T(128)S(6)} %select_n.33), kind=kOutput, calls=%fused_computation.1 | convolution fusion | flops 2164260864 | bytes 60817412 | tf_op jit(solution)/shard_map/rnxsd,rnxsf->xdf/dot_general | solution.py:54
  275.3 14.6 %convolution_convert_fusion = bf16[2,2048,1024]{1,2,0:T(8,128)(2,1)} fusion(bf16[2048,2,1024]{0,2,1:T(8,128)(2,1)} %bitcast.68, bf16[1,2,1024,1024]{3,2,1,0:T(8,128)(2,1)} %param.7), kind=kOutput, calls=%fused_computation.7 | convolution fusion | flops 8594128896 | bytes 20971520 | tf_op jit(solution)/shard_map/xdbk,xbkj->xdbj/dot_general | solution.py:64
  289.9 0.0 slice-done
  289.9 0.0 slice-done.1
  289.9 21.5 %convert_bitcast_fusion = bf16[1,2048,2048]{1,2,0:T(8,128)(2,1)} fusion(bf16[2048,2048]{0,1:T(8,128)(2,1)} %bitcast.69, bf16[1,2048,2048]{2,1,0:T(8,128)(2,1)S(1)} %bitcast.67), kind=kOutput, calls=%fused_computation.6 | convolution fusion | flops 17184063488 | bytes 25165824 | tf_op jit(solution)/shard_map/xde,xef->xdf/dot_general | solution.py:66
  311.5 12.2 %copy.17 = bf16[1,2048,2048]{2,1,0:T(8,128)(2,1)} copy(bf16[1,2048,2048]{1,2,0:T(8,128)(2,1)} %convert_bitcast_fusion) | data formatting | bytes 16777216 | tf_op jit(solution)/shard_map/convert_element_type | solution.py:67
  (1 shorter events, 0.0 us)
Async XLA Ops:
  66.5 18.9 %all-to-all-start.2 = ((bf16[8,1,32,2048]{3,2,1,0:T(8,128)(2,1)}), bf16[8,1,32,2048]{3,2,1,0:T(8,128)(2,1)S(1)}, u32[]{:S(2)}, u32[]{:S(2)}) async-start(bf16[8,1,32,2048]{3,2,1,0:T(8,128)(2,1)} %bitcast.1), calls=%async_computation.2 | async-start | bytes 2097152 | tf_op jit(solution)/shard_map/all_to_all | solution.py:26
  85.4 140.3 %all-to-all-start.1 = ((bf16[1,8,1,32,4,2048]{5,3,1,2,0,4:T(8,128)(2,1)}), bf16[1,8,1,32,4,2048]{5,3,1,2,0,4:T(8,128)(2,1)}, u32[]{:S(2)}, u32[]{:S(2)}) async-start(bf16[1,8,1,32,4,2048]{5,3,1,2,0,4:T(8,128)(2,1)} %copy.14), calls=%async_computation.1 | async-start | bytes 8388608 | tf_op jit(solution)/shard_map/all_to_all | solution.py:17
  90.3 95.5 %collective-permute-start.1 = (bf16[1,8,1,32,2048]{4,3,1,2,0:T(8,128)(2,1)S(1)}, bf16[1,8,1,32,2048]{4,3,1,2,0:T(8,128)(2,1)S(1)}, u32[]{:S(2)}, u32[]{:S(2)}) collective-permute-start(bf16[1,8,1,32,2048]{4,3,1,2,0:T(8,128)(2,1)S(1)} %bitcast.64), channel_id=1, source_target_pairs={{0,1},{1,2},{2,3},{3,0},{4,5},{5,6},{6,7},{7,4},{8,9},{9,10},{10,1... | collective-permute-start | bytes 3145736 | tf_op jit(solution)/shard_map/ppermute | solution.py:43
  92.3 152.1 %collective-permute-start = (bf16[1,8,1,32,2048]{4,3,1,2,0:T(8,128)(2,1)S(1)}, bf16[1,8,1,32,2048]{4,3,1,2,0:T(8,128)(2,1)}, u32[]{:S(2)}, u32[]{:S(2)}) collective-permute-start(bf16[1,8,1,32,2048]{4,3,1,2,0:T(8,128)(2,1)S(1)} %bitcast.65), channel_id=1, source_target_pairs={{0,3},{1,0},{2,1},{3,2},{4,7},{5,4},{6,5},{7,6},{8,11},{9,8},{10,9... | collective-permute-start | bytes 3145736 | tf_op jit(solution)/shard_map/ppermute | solution.py:45
  185.8 68.4 %collective-permute-start.2 = (bf16[1,8,1,32,2048]{4,3,1,2,0:T(8,128)(2,1)S(1)}, bf16[1,8,1,32,2048]{4,3,1,2,0:T(8,128)(2,1)}, u32[]{:S(2)}, u32[]{:S(2)}) collective-permute-start(bf16[1,8,1,32,2048]{4,3,1,2,0:T(8,128)(2,1)S(1)} %collective-permute-done.1), channel_id=1, source_target_pairs={{0,1},{1,2},{2,3},{3,0},{4,5},{5,6},{6,7},{7,4},{8,9},{9,10},{10,1... | collective-permute-start | bytes 3145736 | tf_op jit(solution)/shard_map/ppermute | solution.py:43
  244.4 45.5 %slice-start = ((s8[8388608]{0:T(1024)(128)(4,1)}), s8[4194304]{0:T(1024)(128)(4,1)S(1)}, s32[]{:S(2)}) async-start(s8[8388608]{0:T(1024)(128)(4,1)} %bitcast.66), calls=%async_computation.3 | async-start | bytes 8388608
  254.2 35.7 %slice-start.1 = ((s8[8388608]{0:T(1024)(128)(4,1)}), s8[4194304]{0:T(1024)(128)(4,1)S(1)}, s32[]{:S(2)}) async-start(s8[8388608]{0:T(1024)(128)(4,1)} %bitcast.66), calls=%async_computation.4 | async-start | bytes 8388608
